TPU v7x, 256 devices: a whole 4x4x8 slice. The times are simulated.
256 devices in a mesh: lon: 32 (over z, y_hi, core), lat: 8 (over y_lo, x).
Axes of the slice: x: 4, y: 4 (y_hi: 2, y_lo: 2; y = y_hi * 2 + y_lo), z: 8, core: 2. Of those that a mesh axis runs over, the one named last changes fastest.
Arguments:
- fields: bfloat16 [1024, 1024, 256], P('lat', 'lon'), may hold values from -6 to 6
- spec_weight: bfloat16 [2, 2, 17, 256, 256], replicated, may hold values from -0.75 to 0.75
- skip_weight: bfloat16 [2, 256, 256], replicated, may hold values from -0.375 to 0.375
- diffusion: float32 [2, 256], replicated, may hold values from 0.2 to 1
Outputs:
- result: bfloat16 [1024, 1024, 256], P('lat', 'lon')
All inputs are finite; a program needn't handle non-finite values.
Results may differ from a plain program's by a relative error of at most 0.01.
Values may be sent and summed in bfloat16 or wider, within the bound.
No kernel may reach another device: no remote copies, remote signals or barrier semaphores. Data moves between devices by JAX's collectives and lax.ppermute only.
A program may use at most 128 MiB of HBM per device.

v0:
```python
import math

import jax
import jax.numpy as jnp
import ml_dtypes
import numpy as np
from jax import lax
from jax.experimental import pallas as pl
from jax.experimental.pallas import tpu as pltpu
from jax.sharding import PartitionSpec as P


WINDOW = 64
HOP = 32
MODES = 17
COEFS = 2 * MODES
LANE = 8

BF16 = jnp.bfloat16
F32 = jnp.float32
GELU_A = 2.0 * math.sqrt(2.0 / math.pi)
GELU_B = 4.0 * 0.044715 * GELU_A
VMEM_LIMIT = 16 << 20
SMALL_LIMIT = 4 << 20
CUT_FLOPS = 1 << 31
ROWS = 32

MID = (6, 20)
END = 8


def tables():
    points = np.arange(WINDOW, dtype=np.float64)
    freqs = np.arange(MODES, dtype=np.float64)
    angles = 2.0 * math.pi * points[:, None] * freqs[None, :] / WINDOW
    taper = 0.5 - 0.5 * np.cos(2.0 * math.pi * points / WINDOW)
    analysis = np.concatenate(
        [taper[:, None] * np.cos(angles), -taper[:, None] * np.sin(angles)], axis=1
    )
    factor = np.where(freqs == 0.0, 1.0, 2.0) / WINDOW
    synthesis = np.concatenate(
        [factor[:, None] * np.cos(angles).T, -factor[:, None] * np.sin(angles).T], axis=0
    )
    return analysis, synthesis


def banded(sources, places):
    analysis, synthesis = tables()
    strips = len(sources)
    forward = np.zeros((COEFS, LANE, strips, HOP))
    for n, s in enumerate(sources):
        if s < strips - 1:
            forward[:, s, n] = analysis[:HOP].T
        if s > 0:
            forward[:, s - 1, n] = analysis[HOP:].T
    backward = np.zeros((len(places), HOP, 2, MODES, LANE))
    for n, s in enumerate(places):
        backward[n, :, :, :, s] = synthesis[:, :HOP].T.reshape(HOP, 2, MODES)
        backward[n, :, :, :, s - 1] = synthesis[:, HOP:].T.reshape(HOP, 2, MODES)
    backward = backward.transpose(0, 1, 3, 2, 4)
    return (
        forward.reshape(COEFS * LANE, strips * HOP).astype(ml_dtypes.bfloat16),
        (0.5 * backward.reshape(len(places) * HOP, COEFS * LANE)).astype(ml_dtypes.bfloat16),
    )


def all_tables():
    sets = []
    for own, other, near, far in ((2, 4, 6, 0), (4, 2, 0, 6)):
        first = [p + n for p in (own, other, near, far) for n in range(2)]
        inner = first[:4] + [6 if p else 1 for p in (near, far)]
        second = [p - 1 for p in inner]
        sets.append(banded(first, inner) + banded(second, second[:4]))
    return [np.stack(t) for t in zip(*sets)]


def make_kernel(runs, n_in, edges):
    mid_rows = sum(len(run) - 2 for run in runs)
    out_rows = sum(len(run) - 4 for run in runs)

    def spans(cut):
        at = 0
        for run in runs:
            yield run, at, len(run) - cut
            at += len(run) - cut

    def kernel(info, *refs):
        bufs = refs[:n_in]
        spec, skip, diff, a1, s1, a2, s2 = refs[n_in : n_in + 7]
        outs = refs[n_in + 7 : n_in + 11]
        y, coef, mixed = refs[n_in + 11 :]
        high = info[0]
        core = info[1]
        near_inner = info[2]
        far_inner = info[3]

        def strips(row, *wanted):
            return [bufs[row[b][0]][e, row[b][1]] for b, e in wanted]

        evens = [(b, e) for b in range(4) for e in (core, 1 - core)]

        def window(row):
            return jnp.concatenate(strips(row, *evens), axis=0)

        def inner(row):
            return jnp.concatenate(
                strips(row, *evens[:4], (2, near_inner), (3, far_inner)), axis=0
            )

        def analyse(forward, rows):
            for r in range(0, len(rows), 2):
                two = [
                    jnp.dot(forward[high], get(), preferred_element_type=F32).reshape(
                        COEFS, LANE, 256
                    )
                    for get in rows[r : r + 2]
                ]
                coef[:, r * LANE : (r + 2) * LANE, :] = jnp.concatenate(two, axis=1).astype(BF16)

        def mix(l, rows):
            span = rows * LANE
            for k in range(MODES):
                re = coef[k, :span]
                im = coef[MODES + k, :span]
                wr = spec[l, 0, k]
                wi = spec[l, 1, k]
                parts = [
                    jnp.dot(
                        jnp.concatenate([re, i], axis=1),
                        jnp.concatenate(ws, axis=0),
                        preferred_element_type=F32,
                    ).reshape(rows, LANE, 256)
                    for i, ws in ((-im, (wr, wi)), (im, (wi, wr)))
                ]
                mixed[:rows, k * 2 * LANE : (k + 1) * 2 * LANE, :] = jnp.concatenate(
                    parts, axis=1
                ).astype(BF16)

        def synth(l, backward, get, at, rows, finish):
            local = skip[l] * 0.5
            spread = diff[l : l + 1] * 0.5
            lines = [get(r) for r in range(2)]
            wide = [v.astype(F32) for v in lines]
            for r in range(rows):
                lines.append(get(r + 2))
                wide.append(lines[r + 2].astype(F32))
                mid = wide[r + 1]
                total = jnp.dot(
                    jnp.concatenate([lines[r + 1], backward[high]], axis=1),
                    jnp.concatenate([local, mixed[at + r]], axis=0),
                    preferred_element_type=F32,
                )
                half = total + spread * ((wide[r] - mid) + (wide[r + 2] - mid))
                inside = half * (GELU_A + GELU_B * (half * half))
                finish(at + r, ((mid + half) + half * jnp.tanh(inside)).astype(BF16))

        def first(r, value):
            y[r] = value

        def second(r, value):
            lower = core == 0
            for p in range(2):
                even = value[2 * p * HOP : (2 * p + 1) * HOP]
                odd = value[(2 * p + 1) * HOP : (2 * p + 2) * HOP]
                outs[2 * p][r] = jnp.where(lower, even, odd)
                outs[2 * p + 1][r] = jnp.where(lower, odd, even)

        analyse(a1, [lambda row=row: window(row) for run in runs for row in run[1:-1]])
        mix(0, mid_rows)
        for run, at, rows in spans(2):
            synth(0, s1, lambda r, run=run: inner(run[r]), at, rows, first)

        if edges:
            for n, row in enumerate((0, mid_rows - 1)):

                @pl.when(info[4 + n] == 1)
                def _(row=row):
                    y[row] = jnp.zeros((6 * HOP, 256), BF16)

        inside = [at + r for _, at, rows in spans(2) for r in range(1, rows - 1)]
        analyse(a2, [lambda r=r: y[r] for r in inside])
        mix(1, out_rows)
        for (_, at, rows), (_, start, _) in zip(spans(4), spans(2)):
            synth(1, s2, lambda r, start=start: y[start + r][: 4 * HOP], at, rows, second)

    vmem = pl.BlockSpec(memory_space=pltpu.VMEM)
    frames = 7 * mid_rows + 5 * out_rows
    return pl.pallas_call(
        kernel,
        out_shape=[jax.ShapeDtypeStruct((out_rows, HOP, 256), BF16)] * 4,
        in_specs=[pl.BlockSpec(memory_space=pltpu.SMEM)] + [vmem] * (n_in + 7),
        out_specs=[vmem] * 4,
        scratch_shapes=[
            pltpu.VMEM((mid_rows, 6 * HOP, 256), BF16),
            pltpu.VMEM((COEFS, mid_rows * LANE, 256), BF16),
            pltpu.VMEM((mid_rows, COEFS * LANE, 256), BF16),
        ],
        compiler_params=pltpu.CompilerParams(vmem_limit_bytes=VMEM_LIMIT),
        cost_estimate=pl.CostEstimate(
            flops=frames * (MODES * 8 * 256 * 256 + 2 * COEFS * (WINDOW + HOP) * 256),
            transcendentals=(mid_rows * 6 + out_rows * 4) * HOP * 256,
            bytes_accessed=mid_rows * 8 * HOP * 256 * 2,
        ),
        name="layers",
    )


def cut_middle(info, fields):
    shift, rows = MID

    def kernel(info, fields, *refs):
        outs, sem = refs[:6], refs[6]
        pos = info[0]
        copies = []
        for n, m in enumerate((2, 3, 1, 0)):
            src = fields.at[pl.ds((pos ^ m) * ROWS + shift, rows)]
            copies.append(pltpu.make_async_copy(src, outs[m], sem.at[n]))
        copies.append(pltpu.make_async_copy(fields.at[pl.ds(126, 2)], outs[4], sem.at[4]))
        copies.append(pltpu.make_async_copy(fields.at[pl.ds(0, 2)], outs[5], sem.at[5]))
        for c in copies:
            c.start()
        for c in copies:
            c.wait()

    vmem = pl.BlockSpec(memory_space=pltpu.VMEM)
    piece = jax.ShapeDtypeStruct((rows, HOP, 256), BF16)
    edge = jax.ShapeDtypeStruct((2, HOP, 256), BF16)
    return pl.pallas_call(
        kernel,
        out_shape=[piece] * 4 + [edge] * 2,
        in_specs=[
            pl.BlockSpec(memory_space=pltpu.SMEM),
            pl.BlockSpec(memory_space=pltpu.HBM),
        ],
        out_specs=[vmem] * 6,
        scratch_shapes=[pltpu.SemaphoreType.DMA((6,))],
        cost_estimate=pl.CostEstimate(flops=CUT_FLOPS, transcendentals=0, bytes_accessed=1 << 20),
        compiler_params=pltpu.CompilerParams(vmem_limit_bytes=SMALL_LIMIT),
        name="cut_middle",
    )(info, fields)


def cut_ends(info, fields, above, below):
    def kernel(info, fields, above, below, *refs):
        outs, sem = refs[:4], refs[4]
        pos = info[0]
        waits = []
        for m in (2, 3, 1, 0):
            block = pos ^ m
            start = block * ROWS
            out = outs[m]
            for n, (at, src, edge, beyond, other, last) in enumerate(
                (
                    (2, start, 0, start - 2, above, 0),
                    (END, start + ROWS - END + 2, 2 * END - 2, start + ROWS, below, 3),
                )
            ):
                c = pltpu.make_async_copy(
                    fields.at[pl.ds(src, END - 2)], out.at[pl.ds(at, END - 2)], sem.at[m, n, 0]
                )
                c.start()
                rim = out.at[pl.ds(edge, 2)]
                got = pltpu.make_async_copy(other, rim, sem.at[m, n, 1])

                @pl.when(block == last)
                def _(got=got):
                    got.start()

                @pl.when(block != last)
                def _(beyond=beyond, rim=rim, m=m, n=n):
                    pltpu.make_async_copy(
                        fields.at[pl.ds(beyond, 2)], rim, sem.at[m, n, 1]
                    ).start()

                waits += [c, got]
        for c in waits:
            c.wait()

    vmem = pl.BlockSpec(memory_space=pltpu.VMEM)
    piece = jax.ShapeDtypeStruct((2 * END, HOP, 256), BF16)
    return pl.pallas_call(
        kernel,
        out_shape=[piece] * 4,
        in_specs=[
            pl.BlockSpec(memory_space=pltpu.SMEM),
            pl.BlockSpec(memory_space=pltpu.HBM),
            pl.BlockSpec(memory_space=pl.ANY),
            pl.BlockSpec(memory_space=pl.ANY),
        ],
        out_specs=[vmem] * 4,
        scratch_shapes=[pltpu.SemaphoreType.DMA((4, 2, 2))],
        cost_estimate=pl.CostEstimate(flops=CUT_FLOPS, transcendentals=0, bytes_accessed=1 << 20),
        compiler_params=pltpu.CompilerParams(vmem_limit_bytes=SMALL_LIMIT),
        name="cut_ends",
    )(info, fields, above, below)


def paste(info, pieces, spots, result=None):
    def kernel(info, *refs):
        out, sem = refs[-2], refs[-1]
        copies = []
        for m in range(4):
            for n, (row, count, at) in enumerate(spots):
                dst = out.at[pl.ds((info[0] ^ m) * ROWS + at, count)]
                copies.append(
                    pltpu.make_async_copy(refs[m].at[pl.ds(row, count)], dst, sem.at[m, n])
                )
        for c in copies:
            c.start()
        for c in copies:
            c.wait()

    some = pl.BlockSpec(memory_space=pl.ANY)
    hbm = pl.BlockSpec(memory_space=pltpu.HBM)
    more = () if result is None else (result,)
    return pl.pallas_call(
        kernel,
        out_shape=jax.ShapeDtypeStruct((4 * ROWS, HOP, 256), BF16),
        in_specs=[pl.BlockSpec(memory_space=pltpu.SMEM)] + [some] * 4 + [hbm] * len(more),
        out_specs=hbm,
        input_output_aliases={5: 0} if more else {},
        scratch_shapes=[pltpu.SemaphoreType.DMA((4, len(spots)))],
        compiler_params=pltpu.CompilerParams(vmem_limit_bytes=SMALL_LIMIT),
        name="paste",
    )(info, *pieces, *more)


def load(spec_weight, skip_weight, diffusion, *tables):
    sources = (spec_weight, skip_weight, diffusion, *tables)
    count = len(sources)

    def kernel(*refs):
        sem = refs[2 * count]
        copies = [
            pltpu.make_async_copy(src, dst, sem.at[n])
            for n, (src, dst) in enumerate(zip(refs[:count], refs[count : 2 * count]))
        ]
        for c in copies:
            c.start()
        for c in copies:
            c.wait()

    return pl.pallas_call(
        kernel,
        out_shape=[pltpu.VMEM(v.shape, v.dtype) for v in sources],
        in_specs=[pl.BlockSpec(memory_space=pltpu.HBM)] * count,
        out_specs=[pl.BlockSpec(memory_space=pltpu.VMEM)] * count,
        scratch_shapes=[pltpu.SemaphoreType.DMA((count,))],
        compiler_params=pltpu.CompilerParams(vmem_limit_bytes=SMALL_LIMIT),
        name="load",
    )(*(pltpu.with_memory_space_constraint(v, pltpu.HBM) for v in sources))


def program(fields, spec_weight, skip_weight, diffusion):
    lon = lax.axis_index("lon")
    lat = lax.axis_index("lat")
    n_lon = lax.axis_size("lon")
    n_lat = lax.axis_size("lat")
    pos = lon % 4
    core = pos % 2

    def swap(v, m):
        return lax.ppermute(v, "lon", [(i, i ^ m) for i in range(n_lon)])

    def along(v, low, high):
        pairs = [(i, (i + (low if i % 4 < 2 else high)) % n_lon) for i in range(n_lon)]
        return lax.ppermute(v, "lon", pairs)

    info = jnp.stack(
        [
            pos // 2,
            core,
            jnp.where(pos < 2, core, 1 - core),
            jnp.where(pos < 2, 1 - core, core),
            ((lat == 0) & (pos == 0)).astype(jnp.int32),
            ((lat == n_lat - 1) & (pos == 3)).astype(jnp.int32),
        ]
    ).astype(jnp.int32)
    at = pos.astype(jnp.int32).reshape(1)

    own, one, two, three, tail, head = cut_middle(at, fields)
    above = lax.ppermute(tail, "lat", [(i, i + 1) for i in range(n_lat - 1)])
    below = lax.ppermute(head, "lat", [(i + 1, i) for i in range(n_lat - 1)])
    other_mid = jnp.stack([swap(two, 2), swap(three, 3)])
    own_mid = jnp.stack([own, swap(one, 1)])
    near_mid = along(own_mid, -4, 4)
    far_mid = along(other_mid, 4, -4)

    own, one, two, three = cut_ends(at, fields, above, below)
    other_end = jnp.stack([swap(two, 2), swap(three, 3)])
    own_end = jnp.stack([own, swap(one, 1)])
    near_end = along(own_end, -4, 4)
    far_end = along(other_end, 4, -4)

    mid = (own_mid, other_mid, near_mid, far_mid)
    end = (own_end, other_end, near_end, far_end)
    rest = load(spec_weight, skip_weight, diffusion, *map(jnp.asarray, all_tables()))

    def rows(first, start, count):
        return [[(first + b, r) for b in range(4)] for r in range(start, start + count)]

    outs = make_kernel([rows(0, 0, MID[1])], 4, False)(info, *mid, *rest)
    back_mid = [swap(outs[m], m) if m else outs[m] for m in range(4)]
    runs = [rows(0, 0, END) + rows(4, 0, 4), rows(4, MID[1] - 4, 4) + rows(0, END, END)]
    outs = make_kernel(runs, 8, True)(info, *end, *mid, *rest)
    back_end = [swap(outs[m], m) if m else outs[m] for m in range(4)]

    result = paste(at, back_mid, [(0, ROWS - 2 * END, END)])
    result = paste(at, back_end, [(0, END, 0), (END, END, ROWS - END)], result)
    return result


def solution(mesh):
    in_specs = (P("lat", "lon", None), P(), P(), P())
    out_specs = P("lat", "lon", None)
    return jax.shard_map(program, mesh=mesh, in_specs=in_specs, out_specs=out_specs, check_vma=False)
```

profile of v0, /device:TPU:1, one launch (start us, length us, event | category | flops | bytes accessed | tf_op | source)
XLA Modules:
  0.0 94.6 jit_solution(4396523673649844922)
XLA Ops:
  0.0 0.0 copy-start
  0.0 1.6 %copy-done = bf16[128,32,256]{2,1,0:T(8,128)(2,1)S(1)} copy-done((bf16[128,32,256]{2,1,0:T(8,128)(2,1)S(1)}, bf16[128,32,256]{2,1,0:T(8,128)(2,1)}, u32[]{:S(2)}) %copy-start) | copy-done | bytes 2097176
  1.6 0.6 cut_middle.1
  2.2 3.8 %collective-permute-start.8 = (bf16[20,32,256]{2,1,0:T(8,128)(2,1)S(1)}, bf16[20,32,256]{2,1,0:T(8,128)(2,1)S(1)}, u32[]{:S(2)}, u32[]{:S(2)}) collective-permute-start(bf16[20,32,256]{2,1,0:T(8,128)(2,1)S(1)} %get-tuple-element.38), channel_id=1, source_target_pairs={{0,16},{8,24},{16,0},{24,8},{32,48},{40,56},{48,32},{56,40},{64,80... | collective-permute-start | bytes 983048 | tf_op jit(solution)/shard_map/ppermute | solution.py:363
  6.0 2.6 %collective-permute-start.9 = (bf16[20,32,256]{2,1,0:T(8,128)(2,1)S(1)}, bf16[20,32,256]{2,1,0:T(8,128)(2,1)S(1)}, u32[]{:S(2)}, u32[]{:S(2)}) collective-permute-start(bf16[20,32,256]{2,1,0:T(8,128)(2,1)S(1)} %get-tuple-element.39), channel_id=1, source_target_pairs={{0,24},{8,16},{16,8},{24,0},{32,56},{40,48},{48,40},{56,32},{64,88... | collective-permute-start | bytes 983048 | tf_op jit(solution)/shard_map/ppermute | solution.py:363
  8.6 1.4 %collective-permute-start = (bf16[2,32,256]{2,1,0:T(8,128)(2,1)S(1)}, bf16[2,32,256]{2,1,0:T(8,128)(2,1)S(1)}, u32[]{:S(2)}, u32[]{:S(2)}) collective-permute-start(bf16[2,32,256]{2,1,0:T(8,128)(2,1)S(1)} %get-tuple-element.30), channel_id=1, source_target_pairs={{0,1},{1,2},{2,3},{3,4},{4,5},{5,6},{6,7},{8,9},{9,10},{10,11},{11... | collective-permute-start | bytes 98312 | tf_op jit(solution)/shard_map/ppermute | solution.py:382
  10.0 1.3 %collective-permute-start.1 = (bf16[2,32,256]{2,1,0:T(8,128)(2,1)S(1)}, bf16[2,32,256]{2,1,0:T(8,128)(2,1)S(1)}, u32[]{:S(2)}, u32[]{:S(2)}) collective-permute-start(bf16[2,32,256]{2,1,0:T(8,128)(2,1)S(1)} %get-tuple-element.31), channel_id=1, source_target_pairs={{1,0},{2,1},{3,2},{4,3},{5,4},{6,5},{7,6},{9,8},{10,9},{11,10},{12... | collective-permute-start | bytes 98312 | tf_op jit(solution)/shard_map/ppermute | solution.py:383
  11.3 0.4 collective-permute-start.7
  11.7 0.0 collective-permute-done.above
  11.7 3.2 %collective-permute-done.1.below = bf16[2,32,256]{2,1,0:T(8,128)(2,1)S(1)} collective-permute-done((bf16[2,32,256]{2,1,0:T(8,128)(2,1)S(1)}, bf16[2,32,256]{2,1,0:T(8,128)(2,1)S(1)}, u32[]{:S(2)}, u32[]{:S(2)}) %collective-permute-start.1) | collective-permute-done | bytes 32800 | tf_op jit(solution)/shard_map/ppermute | solution.py:383
  14.9 1.6 %cut_ends.1 = (bf16[16,32,256]{2,1,0:T(8,128)(2,1)S(1)}, bf16[16,32,256]{2,1,0:T(8,128)(2,1)S(1)}, bf16[16,32,256]{2,1,0:T(8,128)(2,1)S(1)}, bf16[16,32,256]{2,1,0:T(8,128)(2,1)S(1)}) custom-call(s32[1]{0:T(128)} %bitcast.info, bf16[128,32,256]{2,1,0:T(8,128)(2,1)S(1)} %copy-done, bf16[2,32,256]{2,1,0:T(8,128)(2,1)S(1)} %collective-permute-done.above, ...), custom_call_target="tpu_custom_call" | custom-call | flops 2147483648 | bytes 1048576 | tf_op jit(solution)/shard_map/cut_ends/pallas_call | solution.py:281
  16.5 1.3 %collective-permute-start.2 = (bf16[16,32,256]{2,1,0:T(8,128)(2,1)S(1)}, bf16[16,32,256]{2,1,0:T(8,128)(2,1)S(1)}, u32[]{:S(2)}, u32[]{:S(2)}) collective-permute-start(bf16[16,32,256]{2,1,0:T(8,128)(2,1)S(1)} %get-tuple-element.33), channel_id=1, source_target_pairs={{0,8},{8,0},{16,24},{24,16},{32,40},{40,32},{48,56},{56,48},{64,72... | collective-permute-start | bytes 786440 | tf_op jit(solution)/shard_map/ppermute | solution.py:363
  17.8 2.5 %collective-permute-start.3 = (bf16[16,32,256]{2,1,0:T(8,128)(2,1)S(1)}, bf16[16,32,256]{2,1,0:T(8,128)(2,1)S(1)}, u32[]{:S(2)}, u32[]{:S(2)}) collective-permute-start(bf16[16,32,256]{2,1,0:T(8,128)(2,1)S(1)} %get-tuple-element.34), channel_id=1, source_target_pairs={{0,16},{8,24},{16,0},{24,8},{32,48},{40,56},{48,32},{56,40},{64,80... | collective-permute-start | bytes 786440 | tf_op jit(solution)/shard_map/ppermute | solution.py:363
  20.2 0.0 collective-permute-done.8
  20.3 0.8 collective-permute-start.4
  21.0 0.6 collective-permute-done.9
  21.7 0.1 pad_maximum_fusion.1.refs_5_.refs_1_
  21.7 1.8 %collective-permute-start.11 = (bf16[2,20,32,256]{3,2,1,0:T(8,128)(2,1)S(1)}, bf16[2,20,32,256]{3,2,1,0:T(8,128)(2,1)S(1)}, u32[]{:S(2)}, u32[]{:S(2)}) collective-permute-start(bf16[2,20,32,256]{3,2,1,0:T(8,128)(2,1)S(1)} %pad_maximum_fusion.1.refs_5_.refs_1_), channel_id=1, source_target_pairs={{0,32},{8,40},{16,240},{24,248},{32,64},{40,72},{48,16},{56,24},{6... | collective-permute-start | bytes 1966088 | tf_op jit(solution)/shard_map/ppermute | solution.py:367
  23.5 0.0 collective-permute-done.7
  23.5 0.1 pad_maximum_fusion.refs_4_.refs_0_
  23.6 4.0 %collective-permute-start.10 = (bf16[2,20,32,256]{3,2,1,0:T(8,128)(2,1)S(1)}, bf16[2,20,32,256]{3,2,1,0:T(8,128)(2,1)S(1)}, u32[]{:S(2)}, u32[]{:S(2)}) collective-permute-start(bf16[2,20,32,256]{3,2,1,0:T(8,128)(2,1)S(1)} %pad_maximum_fusion.refs_4_.refs_0_), channel_id=1, source_target_pairs={{0,224},{8,232},{16,48},{24,56},{32,0},{40,8},{48,80},{56,88},{64,... | collective-permute-start | bytes 1966088 | tf_op jit(solution)/shard_map/ppermute | solution.py:367
  27.6 0.0 collective-permute-done.3
  27.6 5.3 %collective-permute-done.4 = bf16[16,32,256]{2,1,0:T(8,128)(2,1)S(1)} collective-permute-done((bf16[16,32,256]{2,1,0:T(8,128)(2,1)S(1)}, bf16[16,32,256]{2,1,0:T(8,128)(2,1)S(1)}, u32[]{:S(2)}, u32[]{:S(2)}) %collective-permute-start.4) | collective-permute-done | bytes 262176 | tf_op jit(solution)/shard_map/ppermute | solution.py:363
  32.9 0.1 pad_maximum_fusion.3.refs_1_
  33.0 1.7 %collective-permute-start.6 = (bf16[2,16,32,256]{3,2,1,0:T(8,128)(2,1)S(1)}, bf16[2,16,32,256]{3,2,1,0:T(8,128)(2,1)}, u32[]{:S(2)}, u32[]{:S(2)}) collective-permute-start(bf16[2,16,32,256]{3,2,1,0:T(8,128)(2,1)S(1)} %pad_maximum_fusion.3.refs_1_), channel_id=1, source_target_pairs={{0,32},{8,40},{16,240},{24,248},{32,64},{40,72},{48,16},{56,24},{6... | collective-permute-start | bytes 1572872 | tf_op jit(solution)/shard_map/ppermute | solution.py:367
  34.7 0.0 collective-permute-done.2
  34.7 0.8 pad_maximum_fusion.2.refs_0_
  35.6 4.0 %collective-permute-start.5 = (bf16[2,16,32,256]{3,2,1,0:T(8,128)(2,1)}, bf16[2,16,32,256]{3,2,1,0:T(8,128)(2,1)}, u32[]{:S(2)}, u32[]{:S(2)}) collective-permute-start(bf16[2,16,32,256]{3,2,1,0:T(8,128)(2,1)} %pad_maximum_fusion.2.refs_0_), channel_id=1, source_target_pairs={{0,224},{8,232},{16,48},{24,56},{32,0},{40,8},{48,80},{56,88},{64,... | collective-permute-start | bytes 1572872 | tf_op jit(solution)/shard_map/ppermute | solution.py:367
  39.5 0.1 stack.71.info
  39.6 3.9 %load.1 = (bf16[2,2,17,256,256]{4,3,2,1,0:T(8,128)(2,1)S(1)}, bf16[2,256,256]{2,1,0:T(8,128)(2,1)S(1)}, f32[2,256]{1,0:T(2,128)S(1)}, bf16[2,272,256]{2,1,0:T(8,...) custom-call(bf16[2,2,17,256,256]{4,3,2,1,0:T(8,128)(2,1)} %refs_0_.1, ...), custom_call_target="tpu_custom_call" | custom-call | tf_op jit(solution)/shard_map/load/pallas_call | solution.py:343
  43.5 0.0 collective-permute-done.11.refs_7_.refs_3_
  43.5 0.0 collective-permute-done.10.refs_6_.refs_2_
  43.5 8.2 %layers.3 = (bf16[16,32,256]{2,1,0:T(8,128)(2,1)S(1)}, bf16[16,32,256]{2,1,0:T(8,128)(2,1)S(1)}, bf16[16,32,256]{2,1,0:T(8,128)(2,1)S(1)}, bf16[16,32,256]{2,1,0:T(8,128)(2,1)S(1)}) custom-call(s32[6]{0:T(128)S(1)} %stack.71.info, bf16[2,20,32,256]{3,2,1,0:T(8,128)(2,1)S(1)} %pad_maximum_fusion.refs_4_.refs_0_, ...), custom_call_target="tpu_custom_call" | custom-call | flops 2180317184 | bytes 2359296 | tf_op jit(solution)/shard_map/layers/pallas_call | solution.py:402
  51.7 0.5 collective-permute-start.15
  52.2 1.3 %collective-permute-done.6.refs_3_ = bf16[2,16,32,256]{3,2,1,0:T(8,128)(2,1)} collective-permute-done((bf16[2,16,32,256]{3,2,1,0:T(8,128)(2,1)S(1)}, bf16[2,16,32,256]{3,2,1,0:T(8,128)(2,1)}, u32[]{:S(2)}, u32[]{:S(2)}) %collective-permute-start.6) | collective-permute-done | bytes 524320 | tf_op jit(solution)/shard_map/ppermute | solution.py:367
  53.6 0.0 collective-permute-done.5.refs_2_
  53.6 9.6 %layers.2 = (bf16[16,32,256]{2,1,0:T(8,128)(2,1)S(1)}, bf16[16,32,256]{2,1,0:T(8,128)(2,1)S(1)}, bf16[16,32,256]{2,1,0:T(8,128)(2,1)S(1)}, bf16[16,32,256]{2,1,0:T(8,128)(2,1)S(1)}) custom-call(s32[6]{0:T(128)S(1)} %stack.71.info, bf16[2,16,32,256]{3,2,1,0:T(8,128)(2,1)} %pad_maximum_fusion.2.refs_0_, ...), custom_call_target="tpu_custom_call" | custom-call | flops 2328494080 | bytes 2621440 | tf_op jit(solution)/shard_map/layers/pallas_call | solution.py:405
  63.1 1.0 %collective-permute-start.12 = (bf16[16,32,256]{2,1,0:T(8,128)(2,1)S(1)}, bf16[16,32,256]{2,1,0:T(8,128)(2,1)S(1)}, u32[]{:S(2)}, u32[]{:S(2)}) collective-permute-start(bf16[16,32,256]{2,1,0:T(8,128)(2,1)S(1)} %get-tuple-element.48), channel_id=1, source_target_pairs={{0,8},{8,0},{16,24},{24,16},{32,40},{40,32},{48,56},{56,48},{64,72... | collective-permute-start | bytes 786440 | tf_op jit(solution)/shard_map/ppermute | solution.py:363
  64.1 5.8 %collective-permute-start.16 = (bf16[16,32,256]{2,1,0:T(8,128)(2,1)S(1)}, bf16[16,32,256]{2,1,0:T(8,128)(2,1)S(1)}, u32[]{:S(2)}, u32[]{:S(2)}) collective-permute-start(bf16[16,32,256]{2,1,0:T(8,128)(2,1)S(1)} %get-tuple-element.53), channel_id=1, source_target_pairs={{0,16},{8,24},{16,0},{24,8},{32,48},{40,56},{48,32},{56,40},{64,80... | collective-permute-start | bytes 786440 | tf_op jit(solution)/shard_map/ppermute | solution.py:363
  70.0 0.1 collective-permute-start.17
  70.1 3.2 %collective-permute-start.13 = (bf16[16,32,256]{2,1,0:T(8,128)(2,1)S(1)}, bf16[16,32,256]{2,1,0:T(8,128)(2,1)S(1)}, u32[]{:S(2)}, u32[]{:S(2)}) collective-permute-start(bf16[16,32,256]{2,1,0:T(8,128)(2,1)S(1)} %get-tuple-element.49), channel_id=1, source_target_pairs={{0,16},{8,24},{16,0},{24,8},{32,48},{40,56},{48,32},{56,40},{64,80... | collective-permute-start | bytes 786440 | tf_op jit(solution)/shard_map/ppermute | solution.py:363
  73.2 0.0 collective-permute-done.15.refs_1_
  73.2 0.3 collective-permute-start.14
  73.5 3.0 %collective-permute-done.16.refs_2_ = bf16[16,32,256]{2,1,0:T(8,128)(2,1)S(1)} collective-permute-done((bf16[16,32,256]{2,1,0:T(8,128)(2,1)S(1)}, bf16[16,32,256]{2,1,0:T(8,128)(2,1)S(1)}, u32[]{:S(2)}, u32[]{:S(2)}) %collective-permute-start.16) | collective-permute-done | bytes 262176 | tf_op jit(solution)/shard_map/ppermute | solution.py:363
  76.5 5.9 %collective-permute-done.17.refs_3_ = bf16[16,32,256]{2,1,0:T(8,128)(2,1)S(1)} collective-permute-done((bf16[16,32,256]{2,1,0:T(8,128)(2,1)S(1)}, bf16[16,32,256]{2,1,0:T(8,128)(2,1)S(1)}, u32[]{:S(2)}, u32[]{:S(2)}) %collective-permute-start.17) | collective-permute-done | bytes 262176 | tf_op jit(solution)/shard_map/ppermute | solution.py:363
  82.4 1.0 %paste.2.refs_4_ = bf16[128,32,256]{2,1,0:T(8,128)(2,1)} custom-call(s32[1]{0:T(128)} %bitcast.info, bf16[16,32,256]{2,1,0:T(8,128)(2,1)S(1)} %get-tuple-element.51.refs_0_, bf16[16,32,256]{2,1,0:T(8,128)(2,1)S(1)} %collective-permute-done.15.refs_1_, bf16[16,32,256]{2,1,0:T(8,128)(2,1)S(1)} %collective-permute-done.16.refs_2_, ...), custom_call_target="tpu_custom_call" | custom-call | tf_op jit(solution)/shard_map/paste/pallas_call | solution.py:316
  83.4 0.0 collective-permute-done.12.refs_1_
  83.5 4.3 %collective-permute-done.13.refs_2_ = bf16[16,32,256]{2,1,0:T(8,128)(2,1)S(1)} collective-permute-done((bf16[16,32,256]{2,1,0:T(8,128)(2,1)S(1)}, bf16[16,32,256]{2,1,0:T(8,128)(2,1)S(1)}, u32[]{:S(2)}, u32[]{:S(2)}) %collective-permute-start.13) | collective-permute-done | bytes 262176 | tf_op jit(solution)/shard_map/ppermute | solution.py:363
  87.8 5.6 %collective-permute-done.14.refs_3_ = bf16[16,32,256]{2,1,0:T(8,128)(2,1)S(1)} collective-permute-done((bf16[16,32,256]{2,1,0:T(8,128)(2,1)S(1)}, bf16[16,32,256]{2,1,0:T(8,128)(2,1)S(1)}, u32[]{:S(2)}, u32[]{:S(2)}) %collective-permute-start.14) | collective-permute-done | bytes 262176 | tf_op jit(solution)/shard_map/ppermute | solution.py:363
  93.4 1.0 %paste.3 = bf16[128,32,256]{2,1,0:T(8,128)(2,1)} custom-call(s32[1]{0:T(128)} %bitcast.info, bf16[16,32,256]{2,1,0:T(8,128)(2,1)S(1)} %get-tuple-element.47.refs_0_, bf16[16,32,256]{2,1,0:T(8,128)(2,1)S(1)} %collective-permute-done.12.refs_1_, bf16[16,32,256]{2,1,0:T(8,128)(2,1)S(1)} %collective-permute-done.13.refs_2_, ...), custom_call_target="tpu_custom_call", output_to_operand_aliasing={{}: (5, {})} | custom-call | tf_op jit(solution)/shard_map/paste/pallas_call | solution.py:316
Async XLA Ops:
  0.0 1.6 %copy-start = (bf16[128,32,256]{2,1,0:T(8,128)(2,1)S(1)}, bf16[128,32,256]{2,1,0:T(8,128)(2,1)}, u32[]{:S(2)}) copy-start(bf16[128,32,256]{2,1,0:T(8,128)(2,1)} %fields.3) | copy-start | bytes 6291460
  2.2 18.1 %collective-permute-start.8 = (bf16[20,32,256]{2,1,0:T(8,128)(2,1)S(1)}, bf16[20,32,256]{2,1,0:T(8,128)(2,1)S(1)}, u32[]{:S(2)}, u32[]{:S(2)}) collective-permute-start(bf16[20,32,256]{2,1,0:T(8,128)(2,1)S(1)} %get-tuple-element.38), channel_id=1, source_target_pairs={{0,16},{8,24},{16,0},{24,8},{32,48},{40,56},{48,32},{56,40},{64,80... | collective-permute-start | bytes 983048 | tf_op jit(solution)/shard_map/ppermute | solution.py:363
  6.0 15.7 %collective-permute-start.9 = (bf16[20,32,256]{2,1,0:T(8,128)(2,1)S(1)}, bf16[20,32,256]{2,1,0:T(8,128)(2,1)S(1)}, u32[]{:S(2)}, u32[]{:S(2)}) collective-permute-start(bf16[20,32,256]{2,1,0:T(8,128)(2,1)S(1)} %get-tuple-element.39), channel_id=1, source_target_pairs={{0,24},{8,16},{16,8},{24,0},{32,56},{40,48},{48,40},{56,32},{64,88... | collective-permute-start | bytes 983048 | tf_op jit(solution)/shard_map/ppermute | solution.py:363
  8.6 3.1 %collective-permute-start = (bf16[2,32,256]{2,1,0:T(8,128)(2,1)S(1)}, bf16[2,32,256]{2,1,0:T(8,128)(2,1)S(1)}, u32[]{:S(2)}, u32[]{:S(2)}) collective-permute-start(bf16[2,32,256]{2,1,0:T(8,128)(2,1)S(1)} %get-tuple-element.30), channel_id=1, source_target_pairs={{0,1},{1,2},{2,3},{3,4},{4,5},{5,6},{6,7},{8,9},{9,10},{10,11},{11... | collective-permute-start | bytes 98312 | tf_op jit(solution)/shard_map/ppermute | solution.py:382
  10.0 5.0 %collective-permute-start.1 = (bf16[2,32,256]{2,1,0:T(8,128)(2,1)S(1)}, bf16[2,32,256]{2,1,0:T(8,128)(2,1)S(1)}, u32[]{:S(2)}, u32[]{:S(2)}) collective-permute-start(bf16[2,32,256]{2,1,0:T(8,128)(2,1)S(1)} %get-tuple-element.31), channel_id=1, source_target_pairs={{1,0},{2,1},{3,2},{4,3},{5,4},{6,5},{7,6},{9,8},{10,9},{11,10},{12... | collective-permute-start | bytes 98312 | tf_op jit(solution)/shard_map/ppermute | solution.py:383
  11.3 12.2 %collective-permute-start.7 = (bf16[20,32,256]{2,1,0:T(8,128)(2,1)S(1)}, bf16[20,32,256]{2,1,0:T(8,128)(2,1)S(1)}, u32[]{:S(2)}, u32[]{:S(2)}) collective-permute-start(bf16[20,32,256]{2,1,0:T(8,128)(2,1)S(1)} %get-tuple-element.37), channel_id=1, source_target_pairs={{0,8},{8,0},{16,24},{24,16},{32,40},{40,32},{48,56},{56,48},{64,72... | collective-permute-start | bytes 983048 | tf_op jit(solution)/shard_map/ppermute | solution.py:363
  16.5 18.2 %collective-permute-start.2 = (bf16[16,32,256]{2,1,0:T(8,128)(2,1)S(1)}, bf16[16,32,256]{2,1,0:T(8,128)(2,1)S(1)}, u32[]{:S(2)}, u32[]{:S(2)}) collective-permute-start(bf16[16,32,256]{2,1,0:T(8,128)(2,1)S(1)} %get-tuple-element.33), channel_id=1, source_target_pairs={{0,8},{8,0},{16,24},{24,16},{32,40},{40,32},{48,56},{56,48},{64,72... | collective-permute-start | bytes 786440 | tf_op jit(solution)/shard_map/ppermute | solution.py:363
  17.8 9.8 %collective-permute-start.3 = (bf16[16,32,256]{2,1,0:T(8,128)(2,1)S(1)}, bf16[16,32,256]{2,1,0:T(8,128)(2,1)S(1)}, u32[]{:S(2)}, u32[]{:S(2)}) collective-permute-start(bf16[16,32,256]{2,1,0:T(8,128)(2,1)S(1)} %get-tuple-element.34), channel_id=1, source_target_pairs={{0,16},{8,24},{16,0},{24,8},{32,48},{40,56},{48,32},{56,40},{64,80... | collective-permute-start | bytes 786440 | tf_op jit(solution)/shard_map/ppermute | solution.py:363
  20.3 12.7 %collective-permute-start.4 = (bf16[16,32,256]{2,1,0:T(8,128)(2,1)S(1)}, bf16[16,32,256]{2,1,0:T(8,128)(2,1)S(1)}, u32[]{:S(2)}, u32[]{:S(2)}) collective-permute-start(bf16[16,32,256]{2,1,0:T(8,128)(2,1)S(1)} %get-tuple-element.35), channel_id=1, source_target_pairs={{0,24},{8,16},{16,8},{24,0},{32,56},{40,48},{48,40},{56,32},{64,88... | collective-permute-start | bytes 786440 | tf_op jit(solution)/shard_map/ppermute | solution.py:363
  21.7 21.7 %collective-permute-start.11 = (bf16[2,20,32,256]{3,2,1,0:T(8,128)(2,1)S(1)}, bf16[2,20,32,256]{3,2,1,0:T(8,128)(2,1)S(1)}, u32[]{:S(2)}, u32[]{:S(2)}) collective-permute-start(bf16[2,20,32,256]{3,2,1,0:T(8,128)(2,1)S(1)} %pad_maximum_fusion.1.refs_5_.refs_1_), channel_id=1, source_target_pairs={{0,32},{8,40},{16,240},{24,248},{32,64},{40,72},{48,16},{56,24},{6... | collective-permute-start | bytes 1966088 | tf_op jit(solution)/shard_map/ppermute | solution.py:367
  23.6 19.9 %collective-permute-start.10 = (bf16[2,20,32,256]{3,2,1,0:T(8,128)(2,1)S(1)}, bf16[2,20,32,256]{3,2,1,0:T(8,128)(2,1)S(1)}, u32[]{:S(2)}, u32[]{:S(2)}) collective-permute-start(bf16[2,20,32,256]{3,2,1,0:T(8,128)(2,1)S(1)} %pad_maximum_fusion.refs_4_.refs_0_), channel_id=1, source_target_pairs={{0,224},{8,232},{16,48},{24,56},{32,0},{40,8},{48,80},{56,88},{64,... | collective-permute-start | bytes 1966088 | tf_op jit(solution)/shard_map/ppermute | solution.py:367
  33.0 20.6 %collective-permute-start.6 = (bf16[2,16,32,256]{3,2,1,0:T(8,128)(2,1)S(1)}, bf16[2,16,32,256]{3,2,1,0:T(8,128)(2,1)}, u32[]{:S(2)}, u32[]{:S(2)}) collective-permute-start(bf16[2,16,32,256]{3,2,1,0:T(8,128)(2,1)S(1)} %pad_maximum_fusion.3.refs_1_), channel_id=1, source_target_pairs={{0,32},{8,40},{16,240},{24,248},{32,64},{40,72},{48,16},{56,24},{6... | collective-permute-start | bytes 1572872 | tf_op jit(solution)/shard_map/ppermute | solution.py:367
  35.6 18.0 %collective-permute-start.5 = (bf16[2,16,32,256]{3,2,1,0:T(8,128)(2,1)}, bf16[2,16,32,256]{3,2,1,0:T(8,128)(2,1)}, u32[]{:S(2)}, u32[]{:S(2)}) collective-permute-start(bf16[2,16,32,256]{3,2,1,0:T(8,128)(2,1)} %pad_maximum_fusion.2.refs_0_), channel_id=1, source_target_pairs={{0,224},{8,232},{16,48},{24,56},{32,0},{40,8},{48,80},{56,88},{64,... | collective-permute-start | bytes 1572872 | tf_op jit(solution)/shard_map/ppermute | solution.py:367
  51.7 21.5 %collective-permute-start.15 = (bf16[16,32,256]{2,1,0:T(8,128)(2,1)S(1)}, bf16[16,32,256]{2,1,0:T(8,128)(2,1)S(1)}, u32[]{:S(2)}, u32[]{:S(2)}) collective-permute-start(bf16[16,32,256]{2,1,0:T(8,128)(2,1)S(1)} %get-tuple-element.52), channel_id=1, source_target_pairs={{0,8},{8,0},{16,24},{24,16},{32,40},{40,32},{48,56},{56,48},{64,72... | collective-permute-start | bytes 786440 | tf_op jit(solution)/shard_map/ppermute | solution.py:363
  63.1 20.3 %collective-permute-start.12 = (bf16[16,32,256]{2,1,0:T(8,128)(2,1)S(1)}, bf16[16,32,256]{2,1,0:T(8,128)(2,1)S(1)}, u32[]{:S(2)}, u32[]{:S(2)}) collective-permute-start(bf16[16,32,256]{2,1,0:T(8,128)(2,1)S(1)} %get-tuple-element.48), channel_id=1, source_target_pairs={{0,8},{8,0},{16,24},{24,16},{32,40},{40,32},{48,56},{56,48},{64,72... | collective-permute-start | bytes 786440 | tf_op jit(solution)/shard_map/ppermute | solution.py:363
  64.1 12.4 %collective-permute-start.16 = (bf16[16,32,256]{2,1,0:T(8,128)(2,1)S(1)}, bf16[16,32,256]{2,1,0:T(8,128)(2,1)S(1)}, u32[]{:S(2)}, u32[]{:S(2)}) collective-permute-start(bf16[16,32,256]{2,1,0:T(8,128)(2,1)S(1)} %get-tuple-element.53), channel_id=1, source_target_pairs={{0,16},{8,24},{16,0},{24,8},{32,48},{40,56},{48,32},{56,40},{64,80... | collective-permute-start | bytes 786440 | tf_op jit(solution)/shard_map/ppermute | solution.py:363
  70.0 12.5 %collective-permute-start.17 = (bf16[16,32,256]{2,1,0:T(8,128)(2,1)S(1)}, bf16[16,32,256]{2,1,0:T(8,128)(2,1)S(1)}, u32[]{:S(2)}, u32[]{:S(2)}) collective-permute-start(bf16[16,32,256]{2,1,0:T(8,128)(2,1)S(1)} %get-tuple-element.54), channel_id=1, source_target_pairs={{0,24},{8,16},{16,8},{24,0},{32,56},{40,48},{48,40},{56,32},{64,88... | collective-permute-start | bytes 786440 | tf_op jit(solution)/shard_map/ppermute | solution.py:363
  70.1 17.7 %collective-permute-start.13 = (bf16[16,32,256]{2,1,0:T(8,128)(2,1)S(1)}, bf16[16,32,256]{2,1,0:T(8,128)(2,1)S(1)}, u32[]{:S(2)}, u32[]{:S(2)}) collective-permute-start(bf16[16,32,256]{2,1,0:T(8,128)(2,1)S(1)} %get-tuple-element.49), channel_id=1, source_target_pairs={{0,16},{8,24},{16,0},{24,8},{32,48},{40,56},{48,32},{56,40},{64,80... | collective-permute-start | bytes 786440 | tf_op jit(solution)/shard_map/ppermute | solution.py:363
  73.2 20.2 %collective-permute-start.14 = (bf16[16,32,256]{2,1,0:T(8,128)(2,1)S(1)}, bf16[16,32,256]{2,1,0:T(8,128)(2,1)S(1)}, u32[]{:S(2)}, u32[]{:S(2)}) collective-permute-start(bf16[16,32,256]{2,1,0:T(8,128)(2,1)S(1)} %get-tuple-element.50), channel_id=1, source_target_pairs={{0,24},{8,16},{16,8},{24,0},{32,56},{40,48},{48,40},{56,32},{64,88... | collective-permute-start | bytes 786440 | tf_op jit(solution)/shard_map/ppermute | solution.py:363
where the time goes:
time: 94.8 us; the launch traced here: 94.6 us
  starting transfers between devices  36.5 us (39%)
  waiting for transfers between devices  29.4 us (31%)
  Pallas kernels  25.8 us (27%)
  local copies, waits for them, and re-layouts  1.67 us (2%)
  other arithmetic  1.01 us (1%)
    ppermute x12, waiting for transfers between devices, swap(): return lax.ppermute(v, 'lon', [(i, i ^ m) for i in range(n_lon)])  24.8 us
    ppermute x12, starting transfers between devices, swap(): return lax.ppermute(v, 'lon', [(i, i ^ m) for i in range(n_lon)])  22.3 us
    ppermute x4, starting transfers between devices, along(): return lax.ppermute(v, 'lon', pairs)  11.5 us
    pallas_call x1, Pallas kernels, program(): outs = make_kernel(runs, 8, True)(info, *end, *mid, *rest)  9.56 us
    pallas_call x1, Pallas kernels, program(): outs = make_kernel([rows(0, 0, MID[1])], 4, False)(info, *mid, *rest)  8.21 us
    pallas_call x1, Pallas kernels, load(): pl.pallas_call(kernel, out_shape=[pltpu.VMEM(v.shape, v.dtype) for v in s...  3.86 us
    ppermute x1, waiting for transfers between devices, program(): below = lax.ppermute(head, 'lat', [(i + 1, i) for i in range(n_lat - 1)])  3.22 us
    pallas_call x2, Pallas kernels, paste(): pl.pallas_call(kernel, out_shape=jax.ShapeDtypeStruct((4 * ROWS, HOP, 256...  2.02 us
  transfers between devices with their start and end apart: 18, of which 8 were waited for; matrix products, arithmetic and copies ran while one was open for 1% of the time, Pallas kernels for 26%

commit v1 on v0

--- a/solution.py
+++ b/solution.py
@@ -146,10 +146,8 @@
                 wide.append(lines[r + 2].astype(F32))
                 mid = wide[r + 1]
                 total = jnp.dot(
-                    jnp.concatenate([lines[r + 1], backward[high]], axis=1),
-                    jnp.concatenate([local, mixed[at + r]], axis=0),
-                    preferred_element_type=F32,
-                )
+                    lines[r + 1], local, preferred_element_type=F32
+                ) + jnp.dot(backward[high], mixed[at + r], preferred_element_type=F32)
                 half = total + spread * ((wide[r] - mid) + (wide[r + 2] - mid))
                 inside = half * (GELU_A + GELU_B * (half * half))
                 finish(at + r, ((mid + half) + half * jnp.tanh(inside)).astype(BF16))

time: 94.8 us -> 94.7 us (level)
  transfers between devices with their start and end apart: 18 -> 18, of which waited for: 8 -> 8; matrix products, arithmetic and copies ran while one was open for 1% -> 1% of each run, Pallas kernels for 26% -> 25%
where the time goes in v1:
time: 94.7 us; the launch traced here: 94.5 us
  starting transfers between devices  36.5 us (39%)
  waiting for transfers between devices  29.6 us (31%)
  Pallas kernels  25.5 us (27%)
  local copies, waits for them, and re-layouts  1.67 us (2%)
  other arithmetic  1.01 us (1%)
    ppermute x12, waiting for transfers between devices, swap(): return lax.ppermute(v, 'lon', [(i, i ^ m) for i in range(n_lon)])  24.8 us
    ppermute x12, starting transfers between devices, swap(): return lax.ppermute(v, 'lon', [(i, i ^ m) for i in range(n_lon)])  22.3 us
    ppermute x4, starting transfers between devices, along(): return lax.ppermute(v, 'lon', pairs)  11.5 us
    pallas_call x1, Pallas kernels, program(): outs = make_kernel(runs, 8, True)(info, *end, *mid, *rest)  9.48 us
    pallas_call x1, Pallas kernels, program(): outs = make_kernel([rows(0, 0, MID[1])], 4, False)(info, *mid, *rest)  7.99 us
    pallas_call x1, Pallas kernels, load(): pl.pallas_call(kernel, out_shape=[pltpu.VMEM(v.shape, v.dtype) for v in s...  3.86 us
    ppermute x1, waiting for transfers between devices, program(): below = lax.ppermute(head, 'lat', [(i + 1, i) for i in range(n_lat - 1)])  3.22 us
    pallas_call x2, Pallas kernels, paste(): pl.pallas_call(kernel, out_shape=jax.ShapeDtypeStruct((4 * ROWS, HOP, 256...  2.02 us
  transfers between devices with their start and end apart: 18, of which 8 were waited for; matrix products, arithmetic and copies ran while one was open for 1% of the time, Pallas kernels for 25%

profile of v1, /device:TPU:1, one launch (start us, length us, event | category | flops | bytes accessed | tf_op | source)
XLA Modules:
  0.0 94.5 jit_solution(12412292377795810149)
XLA Ops:
  0.0 0.0 copy-start
  0.0 1.6 %copy-done = bf16[128,32,256]{2,1,0:T(8,128)(2,1)S(1)} copy-done((bf16[128,32,256]{2,1,0:T(8,128)(2,1)S(1)}, bf16[128,32,256]{2,1,0:T(8,128)(2,1)}, u32[]{:S(2)}) %copy-start) | copy-done | bytes 2097176
  1.6 0.6 cut_middle.1
  2.2 3.8 %collective-permute-start.8 = (bf16[20,32,256]{2,1,0:T(8,128)(2,1)S(1)}, bf16[20,32,256]{2,1,0:T(8,128)(2,1)S(1)}, u32[]{:S(2)}, u32[]{:S(2)}) collective-permute-start(bf16[20,32,256]{2,1,0:T(8,128)(2,1)S(1)} %get-tuple-element.38), channel_id=1, source_target_pairs={{0,16},{8,24},{16,0},{24,8},{32,48},{40,56},{48,32},{56,40},{64,80... | collective-permute-start | bytes 983048 | tf_op jit(solution)/shard_map/ppermute | solution.py:361
  6.0 2.6 %collective-permute-start.9 = (bf16[20,32,256]{2,1,0:T(8,128)(2,1)S(1)}, bf16[20,32,256]{2,1,0:T(8,128)(2,1)S(1)}, u32[]{:S(2)}, u32[]{:S(2)}) collective-permute-start(bf16[20,32,256]{2,1,0:T(8,128)(2,1)S(1)} %get-tuple-element.39), channel_id=1, source_target_pairs={{0,24},{8,16},{16,8},{24,0},{32,56},{40,48},{48,40},{56,32},{64,88... | collective-permute-start | bytes 983048 | tf_op jit(solution)/shard_map/ppermute | solution.py:361
  8.6 1.4 %collective-permute-start = (bf16[2,32,256]{2,1,0:T(8,128)(2,1)S(1)}, bf16[2,32,256]{2,1,0:T(8,128)(2,1)S(1)}, u32[]{:S(2)}, u32[]{:S(2)}) collective-permute-start(bf16[2,32,256]{2,1,0:T(8,128)(2,1)S(1)} %get-tuple-element.30), channel_id=1, source_target_pairs={{0,1},{1,2},{2,3},{3,4},{4,5},{5,6},{6,7},{8,9},{9,10},{10,11},{11... | collective-permute-start | bytes 98312 | tf_op jit(solution)/shard_map/ppermute | solution.py:380
  10.0 1.3 %collective-permute-start.1 = (bf16[2,32,256]{2,1,0:T(8,128)(2,1)S(1)}, bf16[2,32,256]{2,1,0:T(8,128)(2,1)S(1)}, u32[]{:S(2)}, u32[]{:S(2)}) collective-permute-start(bf16[2,32,256]{2,1,0:T(8,128)(2,1)S(1)} %get-tuple-element.31), channel_id=1, source_target_pairs={{1,0},{2,1},{3,2},{4,3},{5,4},{6,5},{7,6},{9,8},{10,9},{11,10},{12... | collective-permute-start | bytes 98312 | tf_op jit(solution)/shard_map/ppermute | solution.py:381
  11.3 0.4 collective-permute-start.7
  11.7 0.0 collective-permute-done.above
  11.7 3.2 %collective-permute-done.1.below = bf16[2,32,256]{2,1,0:T(8,128)(2,1)S(1)} collective-permute-done((bf16[2,32,256]{2,1,0:T(8,128)(2,1)S(1)}, bf16[2,32,256]{2,1,0:T(8,128)(2,1)S(1)}, u32[]{:S(2)}, u32[]{:S(2)}) %collective-permute-start.1) | collective-permute-done | bytes 32800 | tf_op jit(solution)/shard_map/ppermute | solution.py:381
  14.9 1.6 %cut_ends.1 = (bf16[16,32,256]{2,1,0:T(8,128)(2,1)S(1)}, bf16[16,32,256]{2,1,0:T(8,128)(2,1)S(1)}, bf16[16,32,256]{2,1,0:T(8,128)(2,1)S(1)}, bf16[16,32,256]{2,1,0:T(8,128)(2,1)S(1)}) custom-call(s32[1]{0:T(128)} %bitcast.info, bf16[128,32,256]{2,1,0:T(8,128)(2,1)S(1)} %copy-done, bf16[2,32,256]{2,1,0:T(8,128)(2,1)S(1)} %collective-permute-done.above, ...), custom_call_target="tpu_custom_call" | custom-call | flops 2147483648 | bytes 1048576 | tf_op jit(solution)/shard_map/cut_ends/pallas_call | solution.py:279
  16.5 1.3 %collective-permute-start.2 = (bf16[16,32,256]{2,1,0:T(8,128)(2,1)S(1)}, bf16[16,32,256]{2,1,0:T(8,128)(2,1)S(1)}, u32[]{:S(2)}, u32[]{:S(2)}) collective-permute-start(bf16[16,32,256]{2,1,0:T(8,128)(2,1)S(1)} %get-tuple-element.33), channel_id=1, source_target_pairs={{0,8},{8,0},{16,24},{24,16},{32,40},{40,32},{48,56},{56,48},{64,72... | collective-permute-start | bytes 786440 | tf_op jit(solution)/shard_map/ppermute | solution.py:361
  17.8 2.5 %collective-permute-start.3 = (bf16[16,32,256]{2,1,0:T(8,128)(2,1)S(1)}, bf16[16,32,256]{2,1,0:T(8,128)(2,1)S(1)}, u32[]{:S(2)}, u32[]{:S(2)}) collective-permute-start(bf16[16,32,256]{2,1,0:T(8,128)(2,1)S(1)} %get-tuple-element.34), channel_id=1, source_target_pairs={{0,16},{8,24},{16,0},{24,8},{32,48},{40,56},{48,32},{56,40},{64,80... | collective-permute-start | bytes 786440 | tf_op jit(solution)/shard_map/ppermute | solution.py:361
  20.2 0.0 collective-permute-done.8
  20.3 0.8 collective-permute-start.4
  21.0 0.6 collective-permute-done.9
  21.7 0.1 pad_maximum_fusion.1.refs_5_.refs_1_
  21.7 1.8 %collective-permute-start.11 = (bf16[2,20,32,256]{3,2,1,0:T(8,128)(2,1)S(1)}, bf16[2,20,32,256]{3,2,1,0:T(8,128)(2,1)S(1)}, u32[]{:S(2)}, u32[]{:S(2)}) collective-permute-start(bf16[2,20,32,256]{3,2,1,0:T(8,128)(2,1)S(1)} %pad_maximum_fusion.1.refs_5_.refs_1_), channel_id=1, source_target_pairs={{0,32},{8,40},{16,240},{24,248},{32,64},{40,72},{48,16},{56,24},{6... | collective-permute-start | bytes 1966088 | tf_op jit(solution)/shard_map/ppermute | solution.py:365
  23.5 0.0 collective-permute-done.7
  23.5 0.1 pad_maximum_fusion.refs_4_.refs_0_
  23.6 4.0 %collective-permute-start.10 = (bf16[2,20,32,256]{3,2,1,0:T(8,128)(2,1)S(1)}, bf16[2,20,32,256]{3,2,1,0:T(8,128)(2,1)S(1)}, u32[]{:S(2)}, u32[]{:S(2)}) collective-permute-start(bf16[2,20,32,256]{3,2,1,0:T(8,128)(2,1)S(1)} %pad_maximum_fusion.refs_4_.refs_0_), channel_id=1, source_target_pairs={{0,224},{8,232},{16,48},{24,56},{32,0},{40,8},{48,80},{56,88},{64,... | collective-permute-start | bytes 1966088 | tf_op jit(solution)/shard_map/ppermute | solution.py:365
  27.6 0.0 collective-permute-done.3
  27.6 5.3 %collective-permute-done.4 = bf16[16,32,256]{2,1,0:T(8,128)(2,1)S(1)} collective-permute-done((bf16[16,32,256]{2,1,0:T(8,128)(2,1)S(1)}, bf16[16,32,256]{2,1,0:T(8,128)(2,1)S(1)}, u32[]{:S(2)}, u32[]{:S(2)}) %collective-permute-start.4) | collective-permute-done | bytes 262176 | tf_op jit(solution)/shard_map/ppermute | solution.py:361
  32.9 0.1 pad_maximum_fusion.3.refs_1_
  33.0 1.7 %collective-permute-start.6 = (bf16[2,16,32,256]{3,2,1,0:T(8,128)(2,1)S(1)}, bf16[2,16,32,256]{3,2,1,0:T(8,128)(2,1)}, u32[]{:S(2)}, u32[]{:S(2)}) collective-permute-start(bf16[2,16,32,256]{3,2,1,0:T(8,128)(2,1)S(1)} %pad_maximum_fusion.3.refs_1_), channel_id=1, source_target_pairs={{0,32},{8,40},{16,240},{24,248},{32,64},{40,72},{48,16},{56,24},{6... | collective-permute-start | bytes 1572872 | tf_op jit(solution)/shard_map/ppermute | solution.py:365
  34.7 0.0 collective-permute-done.2
  34.7 0.8 pad_maximum_fusion.2.refs_0_
  35.6 4.0 %collective-permute-start.5 = (bf16[2,16,32,256]{3,2,1,0:T(8,128)(2,1)}, bf16[2,16,32,256]{3,2,1,0:T(8,128)(2,1)}, u32[]{:S(2)}, u32[]{:S(2)}) collective-permute-start(bf16[2,16,32,256]{3,2,1,0:T(8,128)(2,1)} %pad_maximum_fusion.2.refs_0_), channel_id=1, source_target_pairs={{0,224},{8,232},{16,48},{24,56},{32,0},{40,8},{48,80},{56,88},{64,... | collective-permute-start | bytes 1572872 | tf_op jit(solution)/shard_map/ppermute | solution.py:365
  39.5 0.1 stack.71.info
  39.6 3.9 %load.1 = (bf16[2,2,17,256,256]{4,3,2,1,0:T(8,128)(2,1)S(1)}, bf16[2,256,256]{2,1,0:T(8,128)(2,1)S(1)}, f32[2,256]{1,0:T(2,128)S(1)}, bf16[2,272,256]{2,1,0:T(8,...) custom-call(bf16[2,2,17,256,256]{4,3,2,1,0:T(8,128)(2,1)} %refs_0_.1, ...), custom_call_target="tpu_custom_call" | custom-call | tf_op jit(solution)/shard_map/load/pallas_call | solution.py:341
  43.5 0.0 collective-permute-done.11.refs_7_.refs_3_
  43.5 0.0 collective-permute-done.10.refs_6_.refs_2_
  43.5 8.0 %layers.3 = (bf16[16,32,256]{2,1,0:T(8,128)(2,1)S(1)}, bf16[16,32,256]{2,1,0:T(8,128)(2,1)S(1)}, bf16[16,32,256]{2,1,0:T(8,128)(2,1)S(1)}, bf16[16,32,256]{2,1,0:T(8,128)(2,1)S(1)}) custom-call(s32[6]{0:T(128)S(1)} %stack.71.info, bf16[2,20,32,256]{3,2,1,0:T(8,128)(2,1)S(1)} %pad_maximum_fusion.refs_4_.refs_0_, ...), custom_call_target="tpu_custom_call" | custom-call | flops 2180317184 | bytes 2359296 | tf_op jit(solution)/shard_map/layers/pallas_call | solution.py:400
  51.5 0.5 collective-permute-start.15
  52.0 1.6 %collective-permute-done.6.refs_3_ = bf16[2,16,32,256]{3,2,1,0:T(8,128)(2,1)} collective-permute-done((bf16[2,16,32,256]{3,2,1,0:T(8,128)(2,1)S(1)}, bf16[2,16,32,256]{3,2,1,0:T(8,128)(2,1)}, u32[]{:S(2)}, u32[]{:S(2)}) %collective-permute-start.6) | collective-permute-done | bytes 524320 | tf_op jit(solution)/shard_map/ppermute | solution.py:365
  53.6 0.0 collective-permute-done.5.refs_2_
  53.6 9.5 %layers.2 = (bf16[16,32,256]{2,1,0:T(8,128)(2,1)S(1)}, bf16[16,32,256]{2,1,0:T(8,128)(2,1)S(1)}, bf16[16,32,256]{2,1,0:T(8,128)(2,1)S(1)}, bf16[16,32,256]{2,1,0:T(8,128)(2,1)S(1)}) custom-call(s32[6]{0:T(128)S(1)} %stack.71.info, bf16[2,16,32,256]{3,2,1,0:T(8,128)(2,1)} %pad_maximum_fusion.2.refs_0_, ...), custom_call_target="tpu_custom_call" | custom-call | flops 2328494080 | bytes 2621440 | tf_op jit(solution)/shard_map/layers/pallas_call | solution.py:403
  63.0 1.0 %collective-permute-start.12 = (bf16[16,32,256]{2,1,0:T(8,128)(2,1)S(1)}, bf16[16,32,256]{2,1,0:T(8,128)(2,1)S(1)}, u32[]{:S(2)}, u32[]{:S(2)}) collective-permute-start(bf16[16,32,256]{2,1,0:T(8,128)(2,1)S(1)} %get-tuple-element.48), channel_id=1, source_target_pairs={{0,8},{8,0},{16,24},{24,16},{32,40},{40,32},{48,56},{56,48},{64,72... | collective-permute-start | bytes 786440 | tf_op jit(solution)/shard_map/ppermute | solution.py:361
  64.1 5.8 %collective-permute-start.16 = (bf16[16,32,256]{2,1,0:T(8,128)(2,1)S(1)}, bf16[16,32,256]{2,1,0:T(8,128)(2,1)S(1)}, u32[]{:S(2)}, u32[]{:S(2)}) collective-permute-start(bf16[16,32,256]{2,1,0:T(8,128)(2,1)S(1)} %get-tuple-element.53), channel_id=1, source_target_pairs={{0,16},{8,24},{16,0},{24,8},{32,48},{40,56},{48,32},{56,40},{64,80... | collective-permute-start | bytes 786440 | tf_op jit(solution)/shard_map/ppermute | solution.py:361
  69.9 0.1 collective-permute-start.17
  70.0 3.2 %collective-permute-start.13 = (bf16[16,32,256]{2,1,0:T(8,128)(2,1)S(1)}, bf16[16,32,256]{2,1,0:T(8,128)(2,1)S(1)}, u32[]{:S(2)}, u32[]{:S(2)}) collective-permute-start(bf16[16,32,256]{2,1,0:T(8,128)(2,1)S(1)} %get-tuple-element.49), channel_id=1, source_target_pairs={{0,16},{8,24},{16,0},{24,8},{32,48},{40,56},{48,32},{56,40},{64,80... | collective-permute-start | bytes 786440 | tf_op jit(solution)/shard_map/ppermute | solution.py:361
  73.1 0.0 collective-permute-done.15.refs_1_
  73.1 0.3 collective-permute-start.14
  73.4 3.0 %collective-permute-done.16.refs_2_ = bf16[16,32,256]{2,1,0:T(8,128)(2,1)S(1)} collective-permute-done((bf16[16,32,256]{2,1,0:T(8,128)(2,1)S(1)}, bf16[16,32,256]{2,1,0:T(8,128)(2,1)S(1)}, u32[]{:S(2)}, u32[]{:S(2)}) %collective-permute-start.16) | collective-permute-done | bytes 262176 | tf_op jit(solution)/shard_map/ppermute | solution.py:361
  76.5 5.9 %collective-permute-done.17.refs_3_ = bf16[16,32,256]{2,1,0:T(8,128)(2,1)S(1)} collective-permute-done((bf16[16,32,256]{2,1,0:T(8,128)(2,1)S(1)}, bf16[16,32,256]{2,1,0:T(8,128)(2,1)S(1)}, u32[]{:S(2)}, u32[]{:S(2)}) %collective-permute-start.17) | collective-permute-done | bytes 262176 | tf_op jit(solution)/shard_map/ppermute | solution.py:361
  82.4 1.0 %paste.2.refs_4_ = bf16[128,32,256]{2,1,0:T(8,128)(2,1)} custom-call(s32[1]{0:T(128)} %bitcast.info, bf16[16,32,256]{2,1,0:T(8,128)(2,1)S(1)} %get-tuple-element.51.refs_0_, bf16[16,32,256]{2,1,0:T(8,128)(2,1)S(1)} %collective-permute-done.15.refs_1_, bf16[16,32,256]{2,1,0:T(8,128)(2,1)S(1)} %collective-permute-done.16.refs_2_, ...), custom_call_target="tpu_custom_call" | custom-call | tf_op jit(solution)/shard_map/paste/pallas_call | solution.py:314
  83.4 0.0 collective-permute-done.12.refs_1_
  83.4 4.3 %collective-permute-done.13.refs_2_ = bf16[16,32,256]{2,1,0:T(8,128)(2,1)S(1)} collective-permute-done((bf16[16,32,256]{2,1,0:T(8,128)(2,1)S(1)}, bf16[16,32,256]{2,1,0:T(8,128)(2,1)S(1)}, u32[]{:S(2)}, u32[]{:S(2)}) %collective-permute-start.13) | collective-permute-done | bytes 262176 | tf_op jit(solution)/shard_map/ppermute | solution.py:361
  87.7 5.6 %collective-permute-done.14.refs_3_ = bf16[16,32,256]{2,1,0:T(8,128)(2,1)S(1)} collective-permute-done((bf16[16,32,256]{2,1,0:T(8,128)(2,1)S(1)}, bf16[16,32,256]{2,1,0:T(8,128)(2,1)S(1)}, u32[]{:S(2)}, u32[]{:S(2)}) %collective-permute-start.14) | collective-permute-done | bytes 262176 | tf_op jit(solution)/shard_map/ppermute | solution.py:361
  93.3 1.0 %paste.3 = bf16[128,32,256]{2,1,0:T(8,128)(2,1)} custom-call(s32[1]{0:T(128)} %bitcast.info, bf16[16,32,256]{2,1,0:T(8,128)(2,1)S(1)} %get-tuple-element.47.refs_0_, bf16[16,32,256]{2,1,0:T(8,128)(2,1)S(1)} %collective-permute-done.12.refs_1_, bf16[16,32,256]{2,1,0:T(8,128)(2,1)S(1)} %collective-permute-done.13.refs_2_, ...), custom_call_target="tpu_custom_call", output_to_operand_aliasing={{}: (5, {})} | custom-call | tf_op jit(solution)/shard_map/paste/pallas_call | solution.py:314
Async XLA Ops:
  0.0 1.6 %copy-start = (bf16[128,32,256]{2,1,0:T(8,128)(2,1)S(1)}, bf16[128,32,256]{2,1,0:T(8,128)(2,1)}, u32[]{:S(2)}) copy-start(bf16[128,32,256]{2,1,0:T(8,128)(2,1)} %fields.3) | copy-start | bytes 6291460
  2.2 18.1 %collective-permute-start.8 = (bf16[20,32,256]{2,1,0:T(8,128)(2,1)S(1)}, bf16[20,32,256]{2,1,0:T(8,128)(2,1)S(1)}, u32[]{:S(2)}, u32[]{:S(2)}) collective-permute-start(bf16[20,32,256]{2,1,0:T(8,128)(2,1)S(1)} %get-tuple-element.38), channel_id=1, source_target_pairs={{0,16},{8,24},{16,0},{24,8},{32,48},{40,56},{48,32},{56,40},{64,80... | collective-permute-start | bytes 983048 | tf_op jit(solution)/shard_map/ppermute | solution.py:361
  6.0 15.7 %collective-permute-start.9 = (bf16[20,32,256]{2,1,0:T(8,128)(2,1)S(1)}, bf16[20,32,256]{2,1,0:T(8,128)(2,1)S(1)}, u32[]{:S(2)}, u32[]{:S(2)}) collective-permute-start(bf16[20,32,256]{2,1,0:T(8,128)(2,1)S(1)} %get-tuple-element.39), channel_id=1, source_target_pairs={{0,24},{8,16},{16,8},{24,0},{32,56},{40,48},{48,40},{56,32},{64,88... | collective-permute-start | bytes 983048 | tf_op jit(solution)/shard_map/ppermute | solution.py:361
  8.6 3.1 %collective-permute-start = (bf16[2,32,256]{2,1,0:T(8,128)(2,1)S(1)}, bf16[2,32,256]{2,1,0:T(8,128)(2,1)S(1)}, u32[]{:S(2)}, u32[]{:S(2)}) collective-permute-start(bf16[2,32,256]{2,1,0:T(8,128)(2,1)S(1)} %get-tuple-element.30), channel_id=1, source_target_pairs={{0,1},{1,2},{2,3},{3,4},{4,5},{5,6},{6,7},{8,9},{9,10},{10,11},{11... | collective-permute-start | bytes 98312 | tf_op jit(solution)/shard_map/ppermute | solution.py:380
  10.0 5.0 %collective-permute-start.1 = (bf16[2,32,256]{2,1,0:T(8,128)(2,1)S(1)}, bf16[2,32,256]{2,1,0:T(8,128)(2,1)S(1)}, u32[]{:S(2)}, u32[]{:S(2)}) collective-permute-start(bf16[2,32,256]{2,1,0:T(8,128)(2,1)S(1)} %get-tuple-element.31), channel_id=1, source_target_pairs={{1,0},{2,1},{3,2},{4,3},{5,4},{6,5},{7,6},{9,8},{10,9},{11,10},{12... | collective-permute-start | bytes 98312 | tf_op jit(solution)/shard_map/ppermute | solution.py:381
  11.3 12.2 %collective-permute-start.7 = (bf16[20,32,256]{2,1,0:T(8,128)(2,1)S(1)}, bf16[20,32,256]{2,1,0:T(8,128)(2,1)S(1)}, u32[]{:S(2)}, u32[]{:S(2)}) collective-permute-start(bf16[20,32,256]{2,1,0:T(8,128)(2,1)S(1)} %get-tuple-element.37), channel_id=1, source_target_pairs={{0,8},{8,0},{16,24},{24,16},{32,40},{40,32},{48,56},{56,48},{64,72... | collective-permute-start | bytes 983048 | tf_op jit(solution)/shard_map/ppermute | solution.py:361
  16.5 18.2 %collective-permute-start.2 = (bf16[16,32,256]{2,1,0:T(8,128)(2,1)S(1)}, bf16[16,32,256]{2,1,0:T(8,128)(2,1)S(1)}, u32[]{:S(2)}, u32[]{:S(2)}) collective-permute-start(bf16[16,32,256]{2,1,0:T(8,128)(2,1)S(1)} %get-tuple-element.33), channel_id=1, source_target_pairs={{0,8},{8,0},{16,24},{24,16},{32,40},{40,32},{48,56},{56,48},{64,72... | collective-permute-start | bytes 786440 | tf_op jit(solution)/shard_map/ppermute | solution.py:361
  17.8 9.8 %collective-permute-start.3 = (bf16[16,32,256]{2,1,0:T(8,128)(2,1)S(1)}, bf16[16,32,256]{2,1,0:T(8,128)(2,1)S(1)}, u32[]{:S(2)}, u32[]{:S(2)}) collective-permute-start(bf16[16,32,256]{2,1,0:T(8,128)(2,1)S(1)} %get-tuple-element.34), channel_id=1, source_target_pairs={{0,16},{8,24},{16,0},{24,8},{32,48},{40,56},{48,32},{56,40},{64,80... | collective-permute-start | bytes 786440 | tf_op jit(solution)/shard_map/ppermute | solution.py:361
  20.3 12.7 %collective-permute-start.4 = (bf16[16,32,256]{2,1,0:T(8,128)(2,1)S(1)}, bf16[16,32,256]{2,1,0:T(8,128)(2,1)S(1)}, u32[]{:S(2)}, u32[]{:S(2)}) collective-permute-start(bf16[16,32,256]{2,1,0:T(8,128)(2,1)S(1)} %get-tuple-element.35), channel_id=1, source_target_pairs={{0,24},{8,16},{16,8},{24,0},{32,56},{40,48},{48,40},{56,32},{64,88... | collective-permute-start | bytes 786440 | tf_op jit(solution)/shard_map/ppermute | solution.py:361
  21.7 21.7 %collective-permute-start.11 = (bf16[2,20,32,256]{3,2,1,0:T(8,128)(2,1)S(1)}, bf16[2,20,32,256]{3,2,1,0:T(8,128)(2,1)S(1)}, u32[]{:S(2)}, u32[]{:S(2)}) collective-permute-start(bf16[2,20,32,256]{3,2,1,0:T(8,128)(2,1)S(1)} %pad_maximum_fusion.1.refs_5_.refs_1_), channel_id=1, source_target_pairs={{0,32},{8,40},{16,240},{24,248},{32,64},{40,72},{48,16},{56,24},{6... | collective-permute-start | bytes 1966088 | tf_op jit(solution)/shard_map/ppermute | solution.py:365
  23.6 19.9 %collective-permute-start.10 = (bf16[2,20,32,256]{3,2,1,0:T(8,128)(2,1)S(1)}, bf16[2,20,32,256]{3,2,1,0:T(8,128)(2,1)S(1)}, u32[]{:S(2)}, u32[]{:S(2)}) collective-permute-start(bf16[2,20,32,256]{3,2,1,0:T(8,128)(2,1)S(1)} %pad_maximum_fusion.refs_4_.refs_0_), channel_id=1, source_target_pairs={{0,224},{8,232},{16,48},{24,56},{32,0},{40,8},{48,80},{56,88},{64,... | collective-permute-start | bytes 1966088 | tf_op jit(solution)/shard_map/ppermute | solution.py:365
  33.0 20.6 %collective-permute-start.6 = (bf16[2,16,32,256]{3,2,1,0:T(8,128)(2,1)S(1)}, bf16[2,16,32,256]{3,2,1,0:T(8,128)(2,1)}, u32[]{:S(2)}, u32[]{:S(2)}) collective-permute-start(bf16[2,16,32,256]{3,2,1,0:T(8,128)(2,1)S(1)} %pad_maximum_fusion.3.refs_1_), channel_id=1, source_target_pairs={{0,32},{8,40},{16,240},{24,248},{32,64},{40,72},{48,16},{56,24},{6... | collective-permute-start | bytes 1572872 | tf_op jit(solution)/shard_map/ppermute | solution.py:365
  35.6 18.0 %collective-permute-start.5 = (bf16[2,16,32,256]{3,2,1,0:T(8,128)(2,1)}, bf16[2,16,32,256]{3,2,1,0:T(8,128)(2,1)}, u32[]{:S(2)}, u32[]{:S(2)}) collective-permute-start(bf16[2,16,32,256]{3,2,1,0:T(8,128)(2,1)} %pad_maximum_fusion.2.refs_0_), channel_id=1, source_target_pairs={{0,224},{8,232},{16,48},{24,56},{32,0},{40,8},{48,80},{56,88},{64,... | collective-permute-start | bytes 1572872 | tf_op jit(solution)/shard_map/ppermute | solution.py:365
  51.5 21.6 %collective-permute-start.15 = (bf16[16,32,256]{2,1,0:T(8,128)(2,1)S(1)}, bf16[16,32,256]{2,1,0:T(8,128)(2,1)S(1)}, u32[]{:S(2)}, u32[]{:S(2)}) collective-permute-start(bf16[16,32,256]{2,1,0:T(8,128)(2,1)S(1)} %get-tuple-element.52), channel_id=1, source_target_pairs={{0,8},{8,0},{16,24},{24,16},{32,40},{40,32},{48,56},{56,48},{64,72... | collective-permute-start | bytes 786440 | tf_op jit(solution)/shard_map/ppermute | solution.py:361
  63.0 20.3 %collective-permute-start.12 = (bf16[16,32,256]{2,1,0:T(8,128)(2,1)S(1)}, bf16[16,32,256]{2,1,0:T(8,128)(2,1)S(1)}, u32[]{:S(2)}, u32[]{:S(2)}) collective-permute-start(bf16[16,32,256]{2,1,0:T(8,128)(2,1)S(1)} %get-tuple-element.48), channel_id=1, source_target_pairs={{0,8},{8,0},{16,24},{24,16},{32,40},{40,32},{48,56},{56,48},{64,72... | collective-permute-start | bytes 786440 | tf_op jit(solution)/shard_map/ppermute | solution.py:361
  64.1 12.4 %collective-permute-start.16 = (bf16[16,32,256]{2,1,0:T(8,128)(2,1)S(1)}, bf16[16,32,256]{2,1,0:T(8,128)(2,1)S(1)}, u32[]{:S(2)}, u32[]{:S(2)}) collective-permute-start(bf16[16,32,256]{2,1,0:T(8,128)(2,1)S(1)} %get-tuple-element.53), channel_id=1, source_target_pairs={{0,16},{8,24},{16,0},{24,8},{32,48},{40,56},{48,32},{56,40},{64,80... | collective-permute-start | bytes 786440 | tf_op jit(solution)/shard_map/ppermute | solution.py:361
  69.9 12.5 %collective-permute-start.17 = (bf16[16,32,256]{2,1,0:T(8,128)(2,1)S(1)}, bf16[16,32,256]{2,1,0:T(8,128)(2,1)S(1)}, u32[]{:S(2)}, u32[]{:S(2)}) collective-permute-start(bf16[16,32,256]{2,1,0:T(8,128)(2,1)S(1)} %get-tuple-element.54), channel_id=1, source_target_pairs={{0,24},{8,16},{16,8},{24,0},{32,56},{40,48},{48,40},{56,32},{64,88... | collective-permute-start | bytes 786440 | tf_op jit(solution)/shard_map/ppermute | solution.py:361
  70.0 17.7 %collective-permute-start.13 = (bf16[16,32,256]{2,1,0:T(8,128)(2,1)S(1)}, bf16[16,32,256]{2,1,0:T(8,128)(2,1)S(1)}, u32[]{:S(2)}, u32[]{:S(2)}) collective-permute-start(bf16[16,32,256]{2,1,0:T(8,128)(2,1)S(1)} %get-tuple-element.49), channel_id=1, source_target_pairs={{0,16},{8,24},{16,0},{24,8},{32,48},{40,56},{48,32},{56,40},{64,80... | collective-permute-start | bytes 786440 | tf_op jit(solution)/shard_map/ppermute | solution.py:361
  73.1 20.2 %collective-permute-start.14 = (bf16[16,32,256]{2,1,0:T(8,128)(2,1)S(1)}, bf16[16,32,256]{2,1,0:T(8,128)(2,1)S(1)}, u32[]{:S(2)}, u32[]{:S(2)}) collective-permute-start(bf16[16,32,256]{2,1,0:T(8,128)(2,1)S(1)} %get-tuple-element.50), channel_id=1, source_target_pairs={{0,24},{8,16},{16,8},{24,0},{32,56},{40,48},{48,40},{56,32},{64,88... | collective-permute-start | bytes 786440 | tf_op jit(solution)/shard_map/ppermute | solution.py:361
